TPU v7x, 256 devices: a whole 4x4x8 slice. The times are simulated.
256 devices in a mesh: dp: 64 (over x, z_lo, y, core), mp: 4 (over z_hi).
Axes of the slice: x: 4, y: 4, z: 8 (z_hi: 4, z_lo: 2; z = z_hi * 2 + z_lo), core: 2. Of those that a mesh axis runs over, the one named last changes fastest.
Arguments:
- pooled: bfloat16 [16384, 3584], P('dp', 'mp'), may hold values from -4 to 4
- w_out: bfloat16 [3584, 3584], P('mp'), may hold values from -0.028931878 to 0.028931878
- assignments: int32 [16384], P('dp'), may hold values from 0 to 4095
- ema_sums: float32 [4096, 3584], P('mp', 'dp'), may hold values from -0.40089186 to 0.40089186
- ema_counts: float32 [4096], P('mp'), may hold values from 1 to 8
Outputs:
- distances: float32 [16384, 4096], P('dp', 'mp')
- new_sums: float32 [4096, 3584], P('mp', 'dp')
- new_counts: float32 [4096], P('mp')
- new_centroids: bfloat16 [4096, 3584], P('mp', 'dp')
All inputs are finite; a program needn't handle non-finite values.
Results may differ from a plain program's by a relative error of at most 0.0011.
Values may be sent and summed in bfloat16 or wider, within the bound.
No kernel may reach another device: no remote copies, remote signals or barrier semaphores. Data moves between devices by JAX's collectives and lax.ppermute only.
A program may use at most 64 MiB of HBM per device.

v0:
```python
import math
import jax
import jax.numpy as jnp
from jax import lax
from jax.sharding import PartitionSpec as P

EPSILON = 1e-06
EMA_DECAY = 0.9


def copy_for_each(value, axis):
    copies = jnp.broadcast_to(value, (lax.axis_size(axis), *value.shape))
    return lax.all_to_all(copies, axis, split_axis=0, concat_axis=0, tiled=True)


def over_copies(value, axis):
    everything = copy_for_each(value, axis)
    return jnp.sum(everything, axis=0)


def laid_out(pieces, dim):
    lengths = list(pieces.shape[1:])
    lengths[dim] *= pieces.shape[0]
    return jnp.moveaxis(pieces, 0, dim).reshape(lengths)


def collect(value, axis, dim):
    pieces = copy_for_each(value, axis)
    return laid_out(pieces, dim)


def body(pooled, w_out, assignments, ema_sums, ema_counts):
    partial_value = jnp.dot(pooled, w_out, preferred_element_type=jnp.float32)
    share_part = lax.psum_scatter(partial_value, "mp", scatter_dimension=1, tiled=True)
    squares = over_copies(jnp.sum(share_part * share_part, axis=1), "mp")
    inverse_norm = 1.0 / jnp.sqrt(squares + EPSILON)
    share_embedded = (share_part * inverse_norm[:, None]).astype(jnp.bfloat16)
    embedded = collect(share_embedded, "mp", 1)
    local_centers = ema_sums.shape[0]
    doc_rows = embedded.shape[0]
    centers = (ema_sums / ema_counts[:, None]).astype(jnp.bfloat16)
    column_piece = lax.all_gather(centers, "dp", axis=1, tiled=True)
    products = lax.dot_general(
        embedded, column_piece, (((1,), (1,)), ((), ())), preferred_element_type=jnp.float32
    )
    piece_wide = column_piece.astype(jnp.float32)
    center_norms = jnp.sum(piece_wide * piece_wide, axis=1)
    products, center_norms = (products, center_norms)
    embed_wide = embedded.astype(jnp.float32)
    doc_norms = jnp.sum(embed_wide * embed_wide, axis=1)
    distances = doc_norms[:, None] + center_norms[None, :] - 2.0 * products
    first_center = lax.axis_index("mp") * local_centers
    center_ids = first_center + jnp.arange(local_centers, dtype=jnp.int32)
    feature_cols = ema_sums.shape[1]
    every_assign = collect(assignments, "dp", 0)
    own_columns = lax.all_to_all(embedded, "dp", split_axis=1, concat_axis=0, tiled=True)
    shard_count = lax.axis_size("dp")
    group_size = math.gcd(shard_count, max(1, 2048 // doc_rows))
    block_rows = group_size * doc_rows
    turns = shard_count // group_size

    def add_block(block_index, totals):
        sums_now, counts_now = totals
        block_assign = lax.dynamic_slice_in_dim(
            every_assign, block_index * block_rows, block_rows, 0
        )
        block_columns = lax.dynamic_slice_in_dim(
            own_columns, block_index * block_rows, block_rows, 0
        )
        one_hot = (block_assign[None, :] == center_ids[:, None]).astype(jnp.bfloat16)
        sums_now = sums_now + jnp.dot(one_hot, block_columns, preferred_element_type=jnp.float32)
        counts_now = counts_now + jnp.sum(one_hot, axis=1, dtype=jnp.float32)
        return (sums_now, counts_now)

    start_sums = (
        jnp.zeros((local_centers, feature_cols), jnp.float32),
        jnp.zeros((local_centers,), jnp.float32),
    )
    batch_sums, batch_counts = lax.fori_loop(0, turns, add_block, start_sums)
    new_counts = EMA_DECAY * ema_counts + (1.0 - EMA_DECAY) * batch_counts
    new_sums = EMA_DECAY * ema_sums + (1.0 - EMA_DECAY) * batch_sums
    new_centroids = (new_sums / new_counts[:, None]).astype(jnp.bfloat16)
    return (distances, new_sums, new_counts, new_centroids)


def solution(mesh):
    return jax.shard_map(
        body,
        mesh=mesh,
        in_specs=(P("dp", "mp"), P("mp", None), P("dp"), P("mp", "dp"), P("mp")),
        out_specs=(P("dp", "mp"), P("mp", "dp"), P("mp"), P("mp", "dp")),
        check_vma=False,
    )
```

profile of v0, /device:TPU:1, one launch (start us, length us, event | category | flops | bytes accessed | tf_op | source)
XLA Modules:
  0.0 354.5 jit_solution(18194676151146856325)
XLA Ops:
  7.2 1.0 copy-done
  8.2 6.7 %fusion.12 = f32[256,3584]{1,0:T(8,128)} fusion(bf16[256,896]{1,0:T(8,128)(2,1)S(1)} %copy-done, bf16[896,3584]{1,0:T(8,128)(2,1)} %param.8), kind=kOutput, calls=%fused_computation.23 | convolution fusion | flops 1644167168 | bytes 10551296 | tf_op jit(solution)/shard_map/dot_general | solution.py:33
  14.9 78.5 %reduce-scatter.2.cloned.1.call-done = f32[256,896]{1,0:T(8,128)} async-done(((f32[256,3584]{1,0:T(8,128)}), f32[256,896]{1,0:T(8,128)}) %reduce-scatter.2.cloned.1.call-update) | async-done | bytes 917520 | tf_op jit(solution)/shard_map/reduce_scatter | solution.py:34
  93.4 1.3 multiply_reduce_fusion.2
  94.7 11.3 %all_to_all.36 = f32[4,1,256]{2,1,0:T(1,128)S(1)} all-to-all(f32[4,1,256]{2,1,0:T(1,128)S(1)} %broadcast_in_dim.26), channel_id=1, replica_groups=mesh['dp'=64,'mp'=4] {'mp'}, dimensions={0} | all-to-all | bytes 8192 | tf_op jit(solution)/shard_map/all_to_all | solution.py:13
  106.1 1.3 multiply_convert_fusion
  107.7 41.2 %all_to_all.37 = bf16[4,256,896]{1,2,0:T(8,128)(2,1)S(1)} all-to-all(bf16[4,256,896]{1,2,0:T(8,128)(2,1)S(1)} %broadcast_in_dim.27), channel_id=1, replica_groups=mesh['dp'=64,'mp'=4] {'mp'}, dimensions={0} | all-to-all | bytes 3670016 | tf_op jit(solution)/shard_map/all_to_all | solution.py:13
  148.9 40.8 %all_to_all.38 = bf16[256,64,56]{0,2,1:T(8,128)(2,1)} all-to-all(bf16[256,64,56]{0,2,1:T(8,128)(2,1)S(1)} %bitcast.13), channel_id=1, replica_groups=mesh['dp'=64,'mp'=4] {'dp'}, dimensions={1} | all-to-all | bytes 3670016 | tf_op jit(solution)/shard_map/all_to_all | solution.py:56
  190.4 4.7 %all-to-all-start.2 = ((s32[64,1,256]{2,1,0:T(1,128)}), s32[64,1,256]{2,1,0:T(1,128)S(1)}, u32[]{:S(2)}, u32[]{:S(2)}) async-start(s32[64,1,256]{2,1,0:T(1,128)} %broadcast_in_dim.30), calls=%async_computation.3 | async-start | bytes 131072 | tf_op jit(solution)/shard_map/all_to_all | solution.py:13
  195.2 4.7 %copy.20 = bf16[64,256,56]{2,1,0:T(8,128)(2,1)} copy(bf16[64,256,56]{1,2,0:T(8,128)(2,1)} %bitcast.15) | data formatting | bytes 3670016
  199.9 3.3 all-to-all-done.2
  203.2 28.9 %while.16 = (s32[]{:T(128)}, f32[1024,56]{0,1:T(8,128)S(1)}, f32[1024]{0:T(1024)S(1)}, s32[16384]{0:T(1024)S(1)}, bf16[16384,56]{1,0:T(8,128)(2,1)}, /*index=5*/...) while((s32[]{:T(128)}, f32[1024,56]{0,1:T(8,128)S(1)}, f32[1024]{0:T(1024)S(1)}, ...), condition=%wide.region_7.0_spmd.clone, body=%wide.region_5.0_spmd.clone.sunk | while | flops 245483520 | bytes 1044658 | solution.py:79
  203.3 1.0 convert_reduce_fusion.2
  204.2 2.6 fusion.22
  206.9 1.0 convert_reduce_fusion.2
  207.8 2.6 fusion.22
  210.5 1.0 convert_reduce_fusion.2
  211.5 2.6 fusion.22
  214.1 1.0 convert_reduce_fusion.2
  215.1 2.6 fusion.22
  217.7 1.0 convert_reduce_fusion.2
  218.7 2.6 fusion.22
  221.3 1.0 convert_reduce_fusion.2
  222.3 2.6 fusion.22
  225.0 1.0 convert_reduce_fusion.2
  225.9 2.6 fusion.22
  228.6 1.0 convert_reduce_fusion.2
  229.5 2.6 fusion.22
  232.2 0.8 divide_convert_fusion
  233.6 105.9 %all-gather.2.cloned.1.call-done = bf16[1024,3584]{0,1:T(8,128)(2,1)} async-done(((bf16[1024,56]{0,1:T(8,128)(2,1)}), bf16[1024,3584]{0,1:T(8,128)(2,1)}) %all-gather.2.cloned.1.call-update) | async-done | bytes 7340048 | tf_op jit(solution)/shard_map/all_gather | solution.py:42
  339.5 4.7 %multiply_reduce_fusion = f32[1024]{0:T(1024)S(1)} fusion(bf16[1024,3584]{0,1:T(8,128)(2,1)} %all-gather.2.cloned.1.call-done), kind=kLoop, calls=%fused_computation.12 | loop fusion | flops 11009024 | bytes 7344128 | tf_op jit(solution)/shard_map/reduce_sum | solution.py:47
  344.6 3.1 fusion.11
  (49 shorter events, 2.3 us)
Async XLA Ops:
  7.2 1.0 copy-start
  7.2 86.2 %reduce-scatter.2.cloned.1.call-start = ((), (), s32[]{:S(2)}) async-start(), calls=%async_computation.5 | async-start | bytes 4587520 | tf_op jit(solution)/shard_map/reduce_scatter | solution.py:34
  107.7 82.0 %copy-start.5 = (s32[256]{0:T(256)S(1)}, s32[256]{0:T(256)}, u32[]{:S(2)}) copy-start(s32[256]{0:T(256)} %param.9) | copy-start | bytes 3076
  190.4 12.8 %all-to-all-start.2 = ((s32[64,1,256]{2,1,0:T(1,128)}), s32[64,1,256]{2,1,0:T(1,128)S(1)}, u32[]{:S(2)}, u32[]{:S(2)}) async-start(s32[64,1,256]{2,1,0:T(1,128)} %broadcast_in_dim.30), calls=%async_computation.3 | async-start | bytes 131072 | tf_op jit(solution)/shard_map/all_to_all | solution.py:13
  195.1 144.3 %all-gather.2.cloned.1.call-start = ((), (), s32[]{:S(2)}) async-start(), calls=%async_computation.6 | async-start | bytes 7454720 | tf_op jit(solution)/shard_map/all_gather | solution.py:42
  203.2 28.9 %copy-start.3 = (f32[1024]{0:T(1024)S(1)}, f32[1024]{0:T(1024)}, u32[]{:S(2)}) copy-start(f32[1024]{0:T(1024)} %param.11) | copy-start | bytes 12292
  203.2 29.0 %copy-start.2 = (f32[1024,56]{0,1:T(8,128)S(1)}, f32[1024,56]{0,1:T(8,128)}, u32[]{:S(2)}) copy-start(f32[1024,56]{0,1:T(8,128)} %param.10) | copy-start | bytes 688132
  232.2 112.0 %copy-start.4 = (f32[1024]{0:T(1024)}, f32[1024]{0:T(1024)S(1)}, u32[]{:S(2)}) copy-start(f32[1024]{0:T(1024)S(1)} %multiply_add_fusion.1) | copy-start | bytes 12292
  339.5 5.2 %copy-start.1 = (bf16[1024,3584]{0,1:T(8,128)(2,1)S(1)}, bf16[1024,3584]{0,1:T(8,128)(2,1)}, u32[]{:S(2)}) copy-start(bf16[1024,3584]{0,1:T(8,128)(2,1)} %all-gather.2.cloned.1.call-done) | copy-start | bytes 22020100
Sparse Core Ops, SparseCore 0:
  15.0 78.3 reduce-scatter.1
  233.2 106.2 all-gather.1
where the time goes:
time: 355 us
  waiting for transfers between devices  188 us (53%)
  blocking collectives  93.3 us (26%)
  matrix products  30.5 us (9%)
  other arithmetic  16.4 us (5%)
  between operations  14.2 us (4%)
  local copies, waits for them, and re-layouts  7.24 us (2%)
  starting transfers between devices  4.83 us (1%)
    all_gather x1, waiting for transfers between devices, body(): column_piece = lax.all_gather(centers, 'dp', axis=1, tiled=True)  106 us
    reduce_scatter x1, waiting for transfers between devices, body(): lax.psum_scatter(partial_value, 'mp', scatter_dimension=1, tiled=True)  78.5 us
    all_to_all x2, blocking collectives, copy_for_each(): return lax.all_to_all(copies, axis, split_axis=0, concat_axis=0, tiled=True)  52.5 us
    all_to_all x1, blocking collectives, body(): lax.all_to_all(embedded, 'dp', split_axis=1, concat_axis=0, tiled=True)  40.8 us
    dot_general x8, matrix products, add_block(): jnp.dot(one_hot, block_columns, preferred_element_type=jnp.float32)  20.7 us
    reduce_sum x8, other arithmetic, add_block(): counts_now = counts_now + jnp.sum(one_hot, axis=1, dtype=jnp.float32)  7.61 us
  transfers between devices with their start and end apart: 3, of which 3 were waited for; matrix products, arithmetic and copies ran while one was open for 1% of the time, Pallas kernels for 0%

commit v1 on v0

--- a/solution.py
+++ b/solution.py
@@ -3,6 +3,7 @@
 import jax.numpy as jnp
 from jax import lax
 from jax.sharding import PartitionSpec as P
+from jax.lax import all_gather
 
 EPSILON = 1e-06
 EMA_DECAY = 0.9
@@ -39,7 +40,8 @@
     local_centers = ema_sums.shape[0]
     doc_rows = embedded.shape[0]
     centers = (ema_sums / ema_counts[:, None]).astype(jnp.bfloat16)
-    column_piece = lax.all_gather(centers, "dp", axis=1, tiled=True)
+    outcome_arr = all_gather(centers, "dp")
+    column_piece = jnp.concatenate(outcome_arr, axis=1)
     products = lax.dot_general(
         embedded, column_piece, (((1,), (1,)), ((), ())), preferred_element_type=jnp.float32
     )

time: 355 us -> 370 us (1.042)
  local copies, waits for them, and re-layouts: 7.24 us -> 21.3 us
    reshape x0 -> x1, local copies, waits for them, and re-layouts: none -> 7.09 us  [body(): column_piece = jnp.concatenate(outcome_arr, axis=1)]
    unnamed x13 -> x12, local copies, waits for them, and re-layouts: 6.15 us -> 13.2 us
where the time goes in v1:
time: 370 us; the launch traced here: 369 us
  waiting for transfers between devices  188 us (51%)
  blocking collectives  93.3 us (25%)
  matrix products  33.6 us (9%)
  local copies, waits for them, and re-layouts  21.3 us (6%)
  between operations  14.2 us (4%)
  other arithmetic  13.7 us (4%)
  starting transfers between devices  4.83 us (1%)
    all_gather x1, waiting for transfers between devices, body(): outcome_arr = all_gather(centers, 'dp')  106 us
    reduce_scatter x1, waiting for transfers between devices, body(): lax.psum_scatter(partial_value, 'mp', scatter_dimension=1, tiled=True)  78.5 us
    all_to_all x2, blocking collectives, copy_for_each(): return lax.all_to_all(copies, axis, split_axis=0, concat_axis=0, tiled=True)  55.6 us
    all_to_all x1, blocking collectives, body(): lax.all_to_all(embedded, 'dp', split_axis=1, concat_axis=0, tiled=True)  37.7 us
    dot_general x8, matrix products, add_block(): jnp.dot(one_hot, block_columns, preferred_element_type=jnp.float32)  20.8 us
    unnamed x12, local copies, waits for them, and re-layouts  13.2 us
    reduce_sum x8, other arithmetic, add_block(): counts_now = counts_now + jnp.sum(one_hot, axis=1, dtype=jnp.float32)  7.6 us
  transfers between devices with their start and end apart: 3, of which 3 were waited for; matrix products, arithmetic and copies ran while one was open for 1% of the time, Pallas kernels for 0%

profile of v1, /device:TPU:1, one launch (start us, length us, event | category | flops | bytes accessed | tf_op | source)
XLA Modules:
  0.0 369.3 jit_solution(9500113627075388973)
XLA Ops:
  7.2 1.0 copy-done
  8.2 6.7 %fusion.12 = f32[256,3584]{1,0:T(8,128)} fusion(bf16[256,896]{1,0:T(8,128)(2,1)S(1)} %copy-done, bf16[896,3584]{1,0:T(8,128)(2,1)} %param.8), kind=kOutput, calls=%fused_computation.23 | convolution fusion | flops 1644167168 | bytes 10551296 | tf_op jit(solution)/shard_map/dot_general | solution.py:34
  14.9 78.5 %reduce-scatter.2.cloned.1.call-done = f32[256,896]{1,0:T(8,128)} async-done(((f32[256,3584]{1,0:T(8,128)}), f32[256,896]{1,0:T(8,128)}) %reduce-scatter.2.cloned.1.call-update) | async-done | bytes 917520 | tf_op jit(solution)/shard_map/reduce_scatter | solution.py:35
  93.4 1.3 multiply_reduce_fusion.2
  94.7 11.3 %all_to_all.36 = f32[4,1,256]{2,1,0:T(1,128)S(1)} all-to-all(f32[4,1,256]{2,1,0:T(1,128)S(1)} %broadcast_in_dim.26), channel_id=1, replica_groups=mesh['dp'=64,'mp'=4] {'mp'}, dimensions={0} | all-to-all | bytes 8192 | tf_op jit(solution)/shard_map/all_to_all | solution.py:14
  106.1 1.3 multiply_convert_fusion
  107.7 44.3 %all_to_all.37 = bf16[4,256,896]{1,2,0:T(8,128)(2,1)S(1)} all-to-all(bf16[4,256,896]{1,2,0:T(8,128)(2,1)S(1)} %broadcast_in_dim.27), channel_id=1, replica_groups=mesh['dp'=64,'mp'=4] {'mp'}, dimensions={0} | all-to-all | bytes 3670016 | tf_op jit(solution)/shard_map/all_to_all | solution.py:14
  152.0 37.7 %all_to_all.38 = bf16[256,64,56]{0,2,1:T(8,128)(2,1)} all-to-all(bf16[256,64,56]{0,2,1:T(8,128)(2,1)S(1)} %bitcast.24), channel_id=1, replica_groups=mesh['dp'=64,'mp'=4] {'dp'}, dimensions={1} | all-to-all | bytes 3670016 | tf_op jit(solution)/shard_map/all_to_all | solution.py:58
  190.4 4.7 %all-to-all-start.2 = ((s32[64,1,256]{2,1,0:T(1,128)}), s32[64,1,256]{2,1,0:T(1,128)S(1)}, u32[]{:S(2)}, u32[]{:S(2)}) async-start(s32[64,1,256]{2,1,0:T(1,128)} %broadcast_in_dim.30), calls=%async_computation.3 | async-start | bytes 131072 | tf_op jit(solution)/shard_map/all_to_all | solution.py:14
  195.2 4.7 %copy.23 = bf16[64,256,56]{2,1,0:T(8,128)(2,1)} copy(bf16[64,256,56]{1,2,0:T(8,128)(2,1)} %bitcast.27) | data formatting | bytes 3670016
  199.9 3.3 all-to-all-done.2
  203.2 29.1 %while.16 = (s32[]{:T(128)}, f32[1024,56]{0,1:T(8,128)S(1)}, f32[1024]{0:T(1024)S(1)}, s32[16384]{0:T(1024)S(1)}, bf16[16384,56]{1,0:T(8,128)(2,1)}, /*index=5*/...) while((s32[]{:T(128)}, f32[1024,56]{0,1:T(8,128)S(1)}, f32[1024]{0:T(1024)S(1)}, ...), condition=%wide.region_7.0_spmd.clone, body=%wide.region_5.0_spmd.clone.sunk | while | flops 245483520 | bytes 1044650 | solution.py:81
  203.2 2.6 fusion.22
  205.9 1.0 convert_reduce_fusion.2
  206.9 2.6 fusion.22
  209.5 1.0 convert_reduce_fusion.2
  210.5 2.6 fusion.22
  213.1 1.0 convert_reduce_fusion.2
  214.1 2.6 fusion.22
  216.7 1.0 convert_reduce_fusion.2
  217.8 2.6 fusion.22
  220.4 1.0 convert_reduce_fusion.2
  221.4 2.6 fusion.22
  224.0 1.0 convert_reduce_fusion.2
  225.0 2.6 fusion.22
  227.6 1.0 convert_reduce_fusion.2
  228.6 2.6 fusion.22
  233.8 106.0 %all-gather.3.cloned.1.call-done = bf16[65536,56]{0,1:T(8,128)(2,1)} async-done(((bf16[1024,56]{0,1:T(8,128)(2,1)}), bf16[65536,56]{0,1:T(8,128)(2,1)}) %all-gather.3.cloned.1.call-update) | async-done | bytes 7340048 | tf_op jit(solution)/shard_map/all_gather | solution.py:43
  339.8 7.4 %copy.26 = bf16[7,8,64,1024]{3,2,1,0:T(8,128)(2,1)S(1)} copy(bf16[7,8,64,1024]{3,1,2,0:T(8,128)(2,1)} %bitcast.26) | data formatting | bytes 14680064
  347.2 2.0 multiply_reduce_fusion
  349.2 7.1 %copy.20 = bf16[1024,64,56]{0,2,1:T(8,128)(2,1)} copy(bf16[1024,64,56]{0,1,2:T(8,128)(2,1)S(1)} %bitcast.22) | data formatting | bytes 14680064 | tf_op jit(solution)/shard_map/reshape | solution.py:44
  356.3 6.1 %fusion.11 = f32[256,1024]{1,0:T(8,128)} fusion(bf16[256,3584]{0,1:T(8,128)(2,1)S(1)} %bitcast.25, bf16[1024,3584]{0,1:T(8,128)(2,1)} %bitcast.23, f32[1024]{0:T(1024)S(1)} %multiply_reduce_fusion, f32[256]{0:T(256)S(1)} %multiply_reduce_fusion.1), kind=kOutput, calls=%fused_computation.15 | convolution fusion | flops 1879834624 | bytes 10228736 | tf_op jit(solution)/shard_map/dot_general | solution.py:45
  (49 shorter events, 3.7 us)
Async XLA Ops:
  7.2 1.0 copy-start
  7.2 86.2 %reduce-scatter.2.cloned.1.call-start = ((), (), s32[]{:S(2)}) async-start(), calls=%async_computation.5 | async-start | bytes 4587520 | tf_op jit(solution)/shard_map/reduce_scatter | solution.py:35
  14.9 174.8 %copy-start.4 = (s32[256]{0:T(256)S(1)}, s32[256]{0:T(256)}, u32[]{:S(2)}) copy-start(s32[256]{0:T(256)} %param.9) | copy-start | bytes 3076
  190.4 12.8 %all-to-all-start.2 = ((s32[64,1,256]{2,1,0:T(1,128)}), s32[64,1,256]{2,1,0:T(1,128)S(1)}, u32[]{:S(2)}, u32[]{:S(2)}) async-start(s32[64,1,256]{2,1,0:T(1,128)} %broadcast_in_dim.30), calls=%async_computation.3 | async-start | bytes 131072 | tf_op jit(solution)/shard_map/all_to_all | solution.py:14
  195.1 144.6 %all-gather.3.cloned.1.call-start = ((), (), s32[]{:S(2)}) async-start(), calls=%async_computation.6 | async-start | bytes 7454720 | tf_op jit(solution)/shard_map/all_gather | solution.py:43
  203.2 29.2 %copy-start.2 = (f32[1024]{0:T(1024)S(1)}, f32[1024]{0:T(1024)}, u32[]{:S(2)}) copy-start(f32[1024]{0:T(1024)} %param.11) | copy-start | bytes 12292
  203.2 29.2 %copy-start.1 = (f32[1024,56]{0,1:T(8,128)S(1)}, f32[1024,56]{0,1:T(8,128)}, u32[]{:S(2)}) copy-start(f32[1024,56]{0,1:T(8,128)} %param.10) | copy-start | bytes 688132
  232.4 114.8 %copy-start.3 = (f32[1024]{0:T(1024)}, f32[1024]{0:T(1024)S(1)}, u32[]{:S(2)}) copy-start(f32[1024]{0:T(1024)S(1)} %multiply_add_fusion.1) | copy-start | bytes 12292
Sparse Core Ops, SparseCore 0:
  15.0 78.3 reduce-scatter.1
  233.4 106.3 all-gather.2
